TPU v7x, 256 devices: a 2x2x32 block of a 4x8x32 slice. The times are simulated.
256 devices in a mesh: groups: 4 (over y, x), tile: 64 (over z, core).
Axes of the slice: x: 2, y: 2, z: 32, core: 2. Of those that a mesh axis runs over, the one named last changes fastest.
The devices are a block of a 4x8x32 slice.
Arguments:
- tracer: float32 [256, 6, 8, 128, 128], P(('groups', 'tile')), parts along dimension 0, may hold values from -6 to 6
- courant_east: bfloat16 [256, 6, 8, 128, 128], P(('groups', 'tile')), parts along dimension 0, may hold values from -1.5 to 1.5
- courant_north: bfloat16 [256, 6, 8, 128, 128], P(('groups', 'tile')), parts along dimension 0, may hold values from -1.5 to 1.5
- diffusivity: bfloat16 [256, 6, 8, 128, 128], P(('groups', 'tile')), parts along dimension 0, may hold values from 0.049804688 to 5
- seam_table: int32 [6, 4, 3], replicated, may hold values from 0 to 5, as said below
Outputs:
- updated: float32 [256, 6, 8, 128, 128], P(('groups', 'tile')), parts along dimension 0
There are 4 independent parts, one for each index of `groups`. A program takes and returns all parts, laid end to end along the dimension named above; an argument that names none is the same for every part. Nothing has to cross between parts.
Inputs may be any that keep to these rules, and one draw needn't show every extreme that they name: seam_table[p, e] = (q, f, r) names the edge f of panel q != p that borders edge e of panel p, and r is 1 where their edge indices run in opposite directions, 0 otherwise; the 24 edges form 12 pairs whose entries name each other with the same r, as on the faces of a cube ; edge 3 of panel 0 borders edge 3 of panel 1.
All inputs are finite; a program needn't handle non-finite values.
Results may differ from a plain program's by a relative error of at most 0.0003.
Values sent between devices are 32-bit elements; how exact they have to be, the bound alone decides.
A program may use at most 128 MiB of HBM per device.

v0:
```python
import math

import jax
import jax.numpy as jnp
from jax import lax
from jax.sharding import PartitionSpec as P

DEPTH = 2


def padded(block, sides, width):
    for axis, dim in sides:
        count = lax.axis_size(axis)
        forward = [(i, i + 1) for i in range(count - 1)]
        forward.append((count - 1, 0))
        backward = [(target, source) for source, target in forward]
        low = lax.ppermute(
            lax.slice_in_dim(block, block.shape[dim] - width, None, axis=dim), axis, forward
        )
        high = lax.ppermute(lax.slice_in_dim(block, 0, width, axis=dim), axis, backward)
        block = jnp.concatenate([low, block, high], axis=dim)
    return block


def from_behind(value, axis, steps):
    count = lax.axis_size(axis)
    pairs = [(source, (source + steps) % count) for source in range(count)]
    return lax.ppermute(value, axis, pairs)


def edge_strips(panels, rows_deep):
    south_rows = jnp.moveaxis(panels[:, :, :, :rows_deep], 3, 1)
    east_rows = jnp.moveaxis(panels[:, :, ::-1, :][:, :, :rows_deep, :], 2, 1)
    north_rows = jnp.moveaxis(panels[:, :, :, ::-1][:, :, :, :rows_deep], 3, 1)
    west_rows = jnp.moveaxis(panels[:, :, :rows_deep, :], 2, 1)
    return jnp.stack([south_rows, east_rows, north_rows, west_rows], axis=1)


def centered(extended, along):
    kept = extended.shape[along] - 4

    def shifted(offset):
        return lax.slice_in_dim(extended, 2 + offset, 2 + offset + kept, axis=along)

    return (8.0 * (shifted(1) - shifted(-1)) - (shifted(2) - shifted(-2))) / 12.0


def advance(panels, ghosts, courant_east, courant_north, diffusivity):
    west_part = jnp.moveaxis(ghosts[:, 3, ::-1], 1, 2)
    east_part = jnp.moveaxis(ghosts[:, 1], 1, 2)
    south_part = jnp.transpose(ghosts[:, 0, ::-1], (0, 2, 3, 1))
    north_part = jnp.transpose(ghosts[:, 2], (0, 2, 3, 1))
    along_first = jnp.concatenate([west_part, panels, east_part], axis=2)
    along_second = jnp.concatenate([south_part, panels, north_part], axis=3)
    forced = panels - (
        courant_east.astype(jnp.float32) * centered(along_first, 2)
        + courant_north.astype(jnp.float32) * centered(along_second, 3)
    )
    coupling = diffusivity.astype(jnp.float32)
    ratios = []
    partial_values = []
    for height in range(panels.shape[1]):
        diagonal = 1.0 + coupling[:, height]
        if height > 0:
            below = coupling[:, height - 1]
            pivot_value = diagonal + below - below * ratios[-1]
            current = (forced[:, height] + below * partial_values[-1]) / pivot_value
        else:
            pivot_value = diagonal
            current = forced[:, height] / pivot_value
        ratios.append(coupling[:, height] / pivot_value)
        partial_values.append(current)
    solved = [partial_values[-1]]
    for height in range(panels.shape[1] - 2, -1, -1):
        solved.insert(0, partial_values[height] + ratios[height] * solved[0])
    return jnp.stack(solved, axis=1)


def panel_tiles(device, across):
    total = across * across
    tile_offset = jnp.arange(6, dtype=jnp.int32) % 2 * (total // 2 + 1)
    return ((device - tile_offset) % total, tile_offset)


def placement(device, across):
    panel_tile, tile_offset = panel_tiles(device, across)
    row_no = panel_tile // across
    col_no = panel_tile % across
    on_edge = jnp.stack(
        [col_no == 0, row_no == across - 1, col_no == across - 1, row_no == 0], axis=1
    ).reshape(24)
    along_edge = jnp.stack([row_no, col_no, row_no, col_no], axis=1).reshape(24)
    return (on_edge, along_edge, panel_tile, tile_offset)


def device_at(edge_no, spot, across):
    return jnp.where(
        edge_no == 0,
        spot * across,
        jnp.where(
            edge_no == 1,
            (across - 1) * across + spot,
            jnp.where(edge_no == 2, spot * across + across - 1, spot),
        ),
    )


def neighbour_step(edge_no, across):
    return jnp.where(
        edge_no == 0, -1, jnp.where(edge_no == 1, across, jnp.where(edge_no == 2, 1, -across))
    )


def sources(seam_table, own_device, across):
    total = across * across
    on_edge, along_edge, panel_tile, tile_offset = placement(own_device, across)
    flat_table = seam_table.reshape(24, 3)
    ghost_edge = jnp.arange(24, dtype=jnp.int32) % 4
    ghost_panel = jnp.arange(24, dtype=jnp.int32) // 4
    turned_spot = jnp.where(flat_table[:, 2] == 1, across - 1 - along_edge, along_edge)
    far_tile = device_at(flat_table[:, 1], turned_spot, across)
    far_device = (far_tile + jnp.take(tile_offset, flat_table[:, 0])) % total
    near_device = (own_device + neighbour_step(ghost_edge, across)) % total
    source_device = jnp.where(on_edge, far_device, near_device)
    source_block = jnp.where(
        on_edge, flat_table[:, 0] * 4 + flat_table[:, 1], ghost_panel * 4 + (ghost_edge + 2) % 4
    )
    reverse_it = jnp.logical_and(on_edge, flat_table[:, 2] == 1)
    return (on_edge, flat_table, source_device, source_block, reverse_it, panel_tile)


def shards(tracer, courant_east, courant_north, diffusivity, seam_table):
    panels = tracer[0]
    tile_count = lax.axis_size("tile")
    across = math.isqrt(tile_count)
    own_device = lax.axis_index("tile")
    strips = edge_strips(panels, DEPTH)
    blocks = strips.reshape((24,) + strips.shape[2:])
    on_edge, flat_table, source_device, source_block, reverse_it, panel_tile = sources(
        seam_table, own_device, across
    )
    everyone = lax.all_gather(blocks[None], "tile", axis=0, tiled=True)
    picked = jnp.take(
        everyone.reshape((tile_count * 24,) + blocks.shape[1:]),
        source_device * 24 + source_block,
        axis=0,
        mode="clip",
    )
    picked = jnp.where(reverse_it[:, None, None, None], picked[..., ::-1], picked)
    both_rows = jnp.stack([strips[:, 0], strips[:, 2]], axis=0)
    widened = padded(both_rows, (("tile", 0),), 1)
    from_west = from_behind(strips[:, 1], "tile", across)
    from_east = from_behind(strips[:, 3], "tile", -across)
    inside = jnp.stack([widened[0], from_east, widened[3], from_west], axis=1).reshape(blocks.shape)
    ghosts = jnp.where(on_edge[:, None, None, None], picked, inside)
    updated = advance(
        panels, ghosts.reshape(strips.shape), courant_east[0], courant_north[0], diffusivity[0]
    )
    return updated[None]


def solution(mesh):
    placed = (
        P(("groups", "tile"), None, None, None, None),
        P(("groups", "tile"), None, None, None, None),
        P(("groups", "tile"), None, None, None, None),
        P(("groups", "tile"), None, None, None, None),
        P(),
    )
    return jax.shard_map(
        shards,
        mesh=mesh,
        in_specs=placed,
        out_specs=P(("groups", "tile"), None, None, None, None),
        check_vma=False,
    )
```

profile of v0, /device:TPU:37, one launch (start us, length us, event | category | flops | bytes accessed | tf_op | source)
XLA Modules:
  0.0 221.7 jit_solution(18018584469695983660)
XLA Ops:
  6.5 0.0 all-gather.2.cloned.1.call-start
  6.6 1.1 slice_bitcast_fusion
  7.6 5.5 %fusion.51 = (f32[6,8,128,2]{3,2,1,0:T(8,128)}, f32[6,8,128,2]{3,2,1,0:T(8,128)S(1)}) fusion(f32[6,8,128,128]{3,2,1,0:T(8,128)} %bitcast.71), kind=kLoop, calls=%fused_computation.150 | loop fusion | bytes 196608 | tf_op jit(solution)/shard_map/slice | solution.py:34
  13.1 0.1 slice.139
  13.2 0.0 copy-start.3
  13.2 2.4 %copy.57 = f32[6,8,128,2]{2,3,1,0:T(2,128)S(1)} copy(f32[6,8,128,2]{3,2,1,0:T(8,128)} %get-tuple-element.23) | data formatting | bytes 98304
  15.6 0.1 slice.141
  15.7 1.2 copy.56
  16.9 0.1 pad_maximum_fusion.4
  17.0 0.7 copy.46
  17.7 0.1 all-gather.2.cloned.1.call-update
  17.8 8.6 %collective-permute-start.3 = (f32[6,2,8,128]{3,1,2,0:T(2,128)S(1)}, f32[6,2,8,128]{3,1,2,0:T(2,128)S(1)}, u32[]{:S(2)}, u32[]{:S(2)}) collective-permute-start(f32[6,2,8,128]{3,1,2,0:T(2,128)S(1)} %bitcast.82), channel_id=1, source_target_pairs={{0,8},{1,9},{2,10},{3,11},{4,12},{5,13},{6,14},{7,15},{8,16},{9,17... | collective-permute-start | bytes 147464 | tf_op jit(solution)/shard_map/ppermute | solution.py:28
  26.4 2.6 %collective-permute-start = (f32[1,6,2,8,128]{4,3,2,1,0:T(8,128)S(1)}, f32[1,6,2,8,128]{4,3,2,1,0:T(8,128)S(1)}, u32[]{:S(2)}, u32[]{:S(2)}) collective-permute-start(f32[1,6,2,8,128]{4,3,2,1,0:T(8,128)S(1)} %copy.47), channel_id=1, source_target_pairs={{0,1},{1,2},{2,3},{3,4},{4,5},{5,6},{6,7},{7,8},{8,9},{9,10},{10,1... | collective-permute-start | bytes 147464 | tf_op jit(solution)/shard_map/ppermute | solution.py:17
  29.1 9.4 %collective-permute-start.2 = (f32[1,6,2,8,128]{4,3,2,1,0:T(8,128)S(1)}, f32[1,6,2,8,128]{4,3,2,1,0:T(8,128)S(1)}, u32[]{:S(2)}, u32[]{:S(2)}) collective-permute-start(f32[1,6,2,8,128]{4,3,2,1,0:T(8,128)S(1)} %copy.49), channel_id=1, source_target_pairs={{1,0},{2,1},{3,2},{4,3},{5,4},{6,5},{7,6},{8,7},{9,8},{10,9},{11,1... | collective-permute-start | bytes 147464 | tf_op jit(solution)/shard_map/ppermute | solution.py:20
  38.5 5.5 %collective-permute-start.1 = (f32[6,2,8,128]{3,1,2,0:T(2,128)S(1)}, f32[6,2,8,128]{3,1,2,0:T(2,128)S(1)}, u32[]{:S(2)}, u32[]{:S(2)}) collective-permute-start(f32[6,2,8,128]{3,1,2,0:T(2,128)S(1)} %get-tuple-element.21), channel_id=1, source_target_pairs={{0,56},{1,57},{2,58},{3,59},{4,60},{5,61},{6,62},{7,63},{8,0},{9,1... | collective-permute-start | bytes 147464 | tf_op jit(solution)/shard_map/ppermute | solution.py:28
  44.1 0.1 pad_add_fusion.1
  44.2 0.1 reshape.343
  44.2 0.1 broadcast_in_dim.32
  44.4 0.1 pad_add_fusion
  44.4 0.1 reshape.344
  44.5 0.0 copy-done.3
  44.5 0.1 copy.43
  44.6 0.1 reshape.341
  44.7 0.7 gather_fusion
  45.5 3.5 %bitcast_convert_fusion = f32[6,8,128,128]{3,2,1,0:T(8,128)} fusion(bf16[1,6,8,128,128]{4,3,2,1,0:T(8,128)(2,1)} %param.8), kind=kLoop, calls=%fused_computation.32 | loop fusion | flops 786432 | bytes 4718592 | tf_op jit(solution)/shard_map/convert_element_type | solution.py:59
  48.9 0.0 collective-permute-done
  49.0 0.0 collective-permute-done.2
  49.0 0.0 collective-permute-done.3
  49.0 0.0 collective-permute-done.1
  49.0 0.1 pad_maximum_fusion.5
  49.2 125.6 %all-gather.2.cloned.1.call-done = f32[64,24,2,8,128]{4,3,2,1,0:T(8,128)} async-done(((f32[1,24,2,8,128]{4,3,2,1,0:T(8,128)}), f32[64,24,2,8,128]{4,3,2,1,0:T(8,128)}) %all-gather.2.cloned.1.call-update) | async-done | bytes 12582928 | tf_op jit(solution)/shard_map/all_gather | solution.py:142
  174.8 5.1 %gather_fusion.1 = f32[24,2,8,128]{3,2,1,0:T(8,128)S(1)} fusion(f32[1536,2,8,128]{3,2,1,0:T(8,128)} %bitcast.89, s32[1024]{0:T(1024)S(1)} %pad_clamp_fusion), kind=kCustom, calls=%fused_computation.1 | custom fusion | bytes 393312 | tf_op jit(solution)/shard_map/jit(_take)/gather | solution.py:143
  179.9 0.1 rev.11
  180.0 0.1 bitcast_select_fusion
  180.2 1.1 copy.61
  181.2 17.3 %rev.13 = f32[6,1,2,8,128]{2,4,3,0,1:T(8,128)} reverse(f32[6,1,2,8,128]{2,4,3,0,1:T(8,128)S(1)} %copy.61), dimensions={2} | reverse | bytes 98304 | tf_op jit(solution)/shard_map/rev | solution.py:51
  198.5 0.0 copy-start
  198.5 2.2 %copy.60 = f32[6,1,2,8,128]{2,4,3,0,1:T(8,128)} copy(f32[6,1,2,8,128]{4,3,2,1,0:T(8,128)S(1)} %get-tuple-element.25) | data formatting | bytes 98304
  200.8 0.1 rev.12
  200.9 0.5 copy-done
  201.4 0.0 copy-start.1
  201.4 10.0 %fusion.7 = f32[6,8,128,128]{3,2,1,0:T(8,128)S(1)} fusion(f32[6,8,128,128]{3,2,1,0:T(8,128)S(1)} %bitcast.72, f32[6,8,2,128]{3,2,1,0:T(2,128)S(1)} %bitcast.85, f32[6,8,2,128]{3,2,1,0:T(2,128)S(1)} %bitcast.86, f32[6,8,128,2]{3,2,1,0:T(8,128)} %bitcast.73, f32[6,8,128,2]{3,2,1,0:T(8,128)} %bitcast.74, bf16[1,6,8,128,128]{4,3,2,1,0:T(8,128)(2,1)} %param.7, ...), kind=kLoop, calls=%fused_computation.17 | loop fusion | flops 18874368 | bytes 9633792 | tf_op jit(solution)/shard_map/sub | solution.py:55
  211.5 0.0 copy-done.1
  211.5 0.7 fusion.22
  212.1 0.7 add_dynamic-update-slice_fusion
  212.9 0.1 constant_dynamic-update-slice_fusion.5
  213.0 0.1 constant_dynamic-update-slice_fusion.3
  213.1 0.1 constant_dynamic-update-slice_fusion.1
  213.2 0.0 copy-start.2
  213.2 1.7 copy-done.2
  (21 shorter events, 0.4 us)
Async XLA Ops:
  6.5 168.2 %all-gather.2.cloned.1.call-start = ((), (), s32[]{:S(2)}) async-start(), calls=%async_computation | async-start | bytes 12779520 | tf_op jit(solution)/shard_map/all_gather | solution.py:142
  13.2 31.3 %copy-start.3 = (s32[6,4,3]{0,1,2:T(4,128)S(1)}, s32[6,4,3]{0,1,2:T(4,128)}, u32[]{:S(2)}) copy-start(s32[6,4,3]{0,1,2:T(4,128)} %param.9) | copy-start | bytes 868
  17.8 31.2 %collective-permute-start.3 = (f32[6,2,8,128]{3,1,2,0:T(2,128)S(1)}, f32[6,2,8,128]{3,1,2,0:T(2,128)S(1)}, u32[]{:S(2)}, u32[]{:S(2)}) collective-permute-start(f32[6,2,8,128]{3,1,2,0:T(2,128)S(1)} %bitcast.82), channel_id=1, source_target_pairs={{0,8},{1,9},{2,10},{3,11},{4,12},{5,13},{6,14},{7,15},{8,16},{9,17... | collective-permute-start | bytes 147464 | tf_op jit(solution)/shard_map/ppermute | solution.py:28
  26.4 22.5 %collective-permute-start = (f32[1,6,2,8,128]{4,3,2,1,0:T(8,128)S(1)}, f32[1,6,2,8,128]{4,3,2,1,0:T(8,128)S(1)}, u32[]{:S(2)}, u32[]{:S(2)}) collective-permute-start(f32[1,6,2,8,128]{4,3,2,1,0:T(8,128)S(1)} %copy.47), channel_id=1, source_target_pairs={{0,1},{1,2},{2,3},{3,4},{4,5},{5,6},{6,7},{7,8},{8,9},{9,10},{10,1... | collective-permute-start | bytes 147464 | tf_op jit(solution)/shard_map/ppermute | solution.py:17
  29.1 19.9 %collective-permute-start.2 = (f32[1,6,2,8,128]{4,3,2,1,0:T(8,128)S(1)}, f32[1,6,2,8,128]{4,3,2,1,0:T(8,128)S(1)}, u32[]{:S(2)}, u32[]{:S(2)}) collective-permute-start(f32[1,6,2,8,128]{4,3,2,1,0:T(8,128)S(1)} %copy.49), channel_id=1, source_target_pairs={{1,0},{2,1},{3,2},{4,3},{5,4},{6,5},{7,6},{8,7},{9,8},{10,9},{11,1... | collective-permute-start | bytes 147464 | tf_op jit(solution)/shard_map/ppermute | solution.py:20
  38.5 10.5 %collective-permute-start.1 = (f32[6,2,8,128]{3,1,2,0:T(2,128)S(1)}, f32[6,2,8,128]{3,1,2,0:T(2,128)S(1)}, u32[]{:S(2)}, u32[]{:S(2)}) collective-permute-start(f32[6,2,8,128]{3,1,2,0:T(2,128)S(1)} %get-tuple-element.21), channel_id=1, source_target_pairs={{0,56},{1,57},{2,58},{3,59},{4,60},{5,61},{6,62},{7,63},{8,0},{9,1... | collective-permute-start | bytes 147464 | tf_op jit(solution)/shard_map/ppermute | solution.py:28
  198.5 2.9 %copy-start = (f32[1,6,8,128,128]{4,3,2,1,0:T(8,128)S(1)}, f32[1,6,8,128,128]{4,3,2,1,0:T(8,128)}, u32[]{:S(2)}) copy-start(f32[1,6,8,128,128]{4,3,2,1,0:T(8,128)} %param.5) | copy-start | bytes 9437188
  201.4 10.0 %copy-start.1 = (f32[6,8,128,128]{3,2,1,0:T(8,128)S(1)}, f32[6,8,128,128]{3,2,1,0:T(8,128)}, u32[]{:S(2)}) copy-start(f32[6,8,128,128]{3,2,1,0:T(8,128)} %bitcast_convert_fusion) | copy-start | bytes 9437188
  213.2 1.7 copy-start.2
Sparse Core Ops, SparseCore 0:
  17.9 156.8 all-gather.1
where the time goes:
time: 222 us
  waiting for transfers between devices  126 us (57%)
  local copies, waits for them, and re-layouts  40.5 us (18%)
  starting transfers between devices  26.2 us (12%)
  other arithmetic  15.6 us (7%)
  between operations  13.7 us (6%)
    all_gather x1, waiting for transfers between devices, shards(): everyone = lax.all_gather(blocks[None], 'tile', axis=0, tiled=True)  126 us
    rev x1, local copies, waits for them, and re-layouts, advance(): south_part = jnp.transpose(ghosts[:, 0, ::-1], (0, 2, 3, 1))  17.3 us
    ppermute x2, starting transfers between devices, from_behind(): return lax.ppermute(value, axis, pairs)  14.2 us
    sub x1, other arithmetic, advance(): panels - (courant_east.astype(jnp.float32) * centered(along_first, 2) + c...  10 us
    ppermute x1, starting transfers between devices, padded(): lax.ppermute(lax.slice_in_dim(block, 0, width, axis=dim), axis, backward)  9.43 us
    unnamed x18, local copies, waits for them, and re-layouts  9.24 us
    slice x2, local copies, waits for them, and re-layouts, edge_strips(): north_rows = jnp.moveaxis(panels[:, :, :, ::-1][:, :, :, :rows_deep], 3, 1)  5.6 us
    gather x1, local copies, waits for them, and re-layouts, shards(): jnp.take(everyone.reshape((tile_count * 24,) + blocks.shape[1:]), source_...  5.14 us
  transfers between devices with their start and end apart: 5, of which 1 were waited for; matrix products, arithmetic and copies ran while one was open for 2% of the time, Pallas kernels for 0%

commit v1 on v0

v1 whole, which is shorter than its diff:
```python
import functools
import math

import jax
import jax.numpy as jnp
from jax import lax
from jax.experimental import pallas as pl
from jax.experimental.pallas import tpu as pltpu
from jax.sharding import PartitionSpec as P

MESH = pl.DeviceIdType.MESH
PAD = 8


class Plan:
    def __init__(self, count):
        self.count = count
        self.side = math.isqrt(count)
        self.shift = count // 2 + 1
        taken = []
        for group in range(self.side // 2):
            members = {
                self.site(par, edge, spot)
                for par in range(2)
                for edge in range(4)
                for spot in (group, self.side - 1 - group)
            }
            free = (d for d in range(1, count, 2) if d not in members and d not in taken)
            taken.append(next(free))
        self.hubs = taken

    def site(self, par, edge, spot):
        side = self.side
        tile = (spot * side, (side - 1) * side + spot, spot * side + side - 1, spot)[edge]
        return (tile + self.shift * par) % self.count

    def hub_of(self, group):
        found = self.hubs[0]
        for i, hub in enumerate(self.hubs):
            if i:
                found = jnp.where(group == i, hub, found)
        return found


def kernel(
    plan, dims,
    tracer, east, north, diff, seam, out,
    q, ce, cn, df, fv, wv, vv, bv, rv,
    strips, turned, ghosts, held, chosen, gi, xb, tt,
    load_sem, coef_sem, send_sem, ghost_sem, held_sem, chosen_sem,
):
    panels, levels, size = dims
    count, side = plan.count, plan.side
    block = levels * size
    me = lax.axis_index("tile")
    half = panels // 2

    def device(d):
        return {"tile": d}

    tiles = [lax.rem(me + (count - plan.shift) * par, count) for par in range(2)]
    rows = [t // side for t in tiles]
    cols = [lax.rem(t, side) for t in tiles]
    on_edge, other, slot, hub, near = {}, {}, {}, {}, {}
    for par in range(2):
        for edge in range(4):
            key = par, edge
            on_edge[key] = (
                cols[par] == 0, rows[par] == side - 1, cols[par] == side - 1, rows[par] == 0
            )[edge]
            spot = (rows, cols, rows, cols)[edge][par]
            group = jnp.minimum(spot, side - 1 - spot)
            other[key] = jnp.where(spot == group, 0, 1)
            slot[key] = (par * 4 + edge) * 2 + other[key]
            hub[key] = plan.hub_of(group)
            near[key] = lax.rem(me + (count - 1, side, 1, count - side)[edge], count)

    barrier = pltpu.get_barrier_semaphore()
    for key in on_edge:
        @pl.when(jnp.logical_not(on_edge[key]))
        def _(key=key):
            pl.semaphore_signal(
                barrier, inc=1, device_id=device(near[key]), device_id_type=MESH
            )
    for group, hub_device in enumerate(plan.hubs):
        @pl.when(me == hub_device)
        def _(group=group):
            for par in range(2):
                for edge in range(4):
                    for spot in (group, side - 1 - group):
                        pl.semaphore_signal(
                            barrier, inc=1, device_id=device(plan.site(par, edge, spot)),
                            device_id_type=MESH,
                        )

    loads = []
    for p in range(panels):
        load = pltpu.make_async_copy(
            tracer.at[pl.ds(p * block, block)], q.at[pl.ds(PAD + p * block, block)],
            load_sem.at[p],
        )
        load.start()
        loads.append(load)
    coefs = []
    for p in range(panels):
        for i, (far, close) in enumerate(((east, ce), (north, cn), (diff, df))):
            load = pltpu.make_async_copy(
                far.at[pl.ds(p * block, block)], close.at[pl.ds(p * block, block)],
                coef_sem.at[p, i],
            )
            load.start()
            coefs.append(load)

    zero = jnp.zeros((8, size), jnp.float32)
    q[pl.ds(0, PAD), :] = zero
    q[pl.ds(PAD + panels * block, PAD), :] = zero
    gi[...] = jnp.zeros(gi.shape, jnp.float32)
    xb[...] = jnp.zeros(xb.shape, jnp.float32)
    lane = lax.broadcasted_iota(jnp.int32, (8, size), 1)
    back = size - 1 - lax.broadcasted_iota(jnp.int32, (2 * levels, size), 1)

    for p in range(panels):
        par, idx = p % 2, p // 2
        first = PAD + p * block
        loads[p].wait()

        def gather(i, carry):
            packed = jnp.zeros((8, size), jnp.float32)
            for k in range(levels):
                row = pl.multiple_of(first + k * size + i * 8, 8)
                moved = pltpu.roll(q[pl.ds(row, 8), :], 4 * k + 2, 1)
                packed = jnp.where(lane // 4 == k, moved, packed)
            tt[p, pl.ds(pl.multiple_of(i * 8, 8), 8), :] = packed
            return carry

        lax.fori_loop(0, size // 8, gather, 0, unroll=4)
        tt[p] = jnp.transpose(tt[p])
        for d in range(2):
            part = pl.ds(d * levels, levels)
            strips[par, 0, idx, part, :] = tt[p, pl.ds(2 + d, levels, stride=4), :]
            strips[par, 2, idx, part, :] = tt[p, pl.ds(1 - d, levels, stride=4), :]
            strips[par, 3, idx, part, :] = q[pl.ds(first + d, levels, stride=size), :]
            strips[par, 1, idx, part, :] = q[pl.ds(first + size - 1 - d, levels, stride=size), :]
        for edge in range(4):
            plain = strips[par, edge, idx]
            flipped = jnp.take_along_axis(plain, back, axis=1)
            turn = seam[2, edge, p]
            turned[par, edge, idx] = jnp.where(turn == 1, flipped, plain)

    def to_hub(key):
        par, edge = key
        return pltpu.make_async_remote_copy(
            turned.at[par, edge], held.at[pl.ds(slot[key] * half, half)],
            send_sem.at[par * 4 + edge], held_sem.at[slot[key]],
            device_id=device(hub[key]), device_id_type=MESH,
        )

    def to_near(key):
        par, edge = key
        return pltpu.make_async_remote_copy(
            strips.at[par, edge], ghosts.at[par, (edge + 2) % 4],
            send_sem.at[par * 4 + edge], ghost_sem.at[par * 4 + (edge + 2) % 4],
            device_id=device(near[key]), device_id_type=MESH,
        )

    pl.semaphore_wait(barrier, 8)
    for key in on_edge:
        @pl.when(on_edge[key])
        def _(key=key):
            to_hub(key).start()

        @pl.when(jnp.logical_not(on_edge[key]))
        def _(key=key):
            to_near(key).start()

    twelfth = 1.0 / 12.0
    wide = lax.broadcasted_iota(jnp.int32, (16, size), 1)
    edge_lane = jnp.logical_or(wide < 2, wide >= size - 2)

    for p in range(panels):
        for load in coefs[3 * p : 3 * p + 3]:
            load.wait()

        def prepare(i, carry):
            before = ratio = None
            for k in range(levels):
                row = pl.multiple_of(p * block + k * size + i * 16, 16)
                here = pl.ds(row, 16)
                mid = q[pl.ds(row + PAD, 16), :]
                di = 8.0 * (q[pl.ds(row + PAD + 1, 16), :] - q[pl.ds(row + PAD - 1, 16), :]) - (
                    q[pl.ds(row + PAD + 2, 16), :] - q[pl.ds(row + PAD - 2, 16), :]
                )
                dj = 8.0 * (pltpu.roll(mid, size - 1, 1) - pltpu.roll(mid, 1, 1)) - (
                    pltpu.roll(mid, size - 2, 1) - pltpu.roll(mid, 2, 1)
                )
                e = ce[here, :].astype(jnp.float32) * twelfth
                n = cn[here, :].astype(jnp.float32) * twelfth
                c = df[here, :].astype(jnp.float32)
                pivot = 1.0 + c
                if k:
                    pivot = pivot + before * (1.0 - ratio)
                inv = 1.0 / pivot
                fv[here, :] = (mid - (e * di + n * dj)) * inv
                wv[here, :] = jnp.where(edge_lane, n * inv, 0.0)
                vv[here, :] = e * inv
                if k:
                    bv[here, :] = before * inv
                ratio = c * inv
                rv[here, :] = ratio
                before = c
            return carry

        lax.fori_loop(0, size // 16, prepare, 0)

    for group, hub_device in enumerate(plan.hubs):
        @pl.when(me == hub_device)
        def _(group=group):
            sites = [
                (par, edge, hi) for par in range(2) for edge in range(4) for hi in range(2)
            ]

            def to_site(number):
                par, edge, hi = sites[number]
                target = plan.site(par, edge, side - 1 - group if hi else group)
                return pltpu.make_async_remote_copy(
                    chosen.at[pl.ds(number * half, half)], ghosts.at[par, edge],
                    chosen_sem.at[number], ghost_sem.at[par * 4 + edge],
                    device_id=device(target), device_id_type=MESH,
                )

            for number in range(len(sites)):
                pltpu.make_async_remote_copy(
                    held.at[pl.ds(number * half, half)], held.at[pl.ds(number * half, half)],
                    chosen_sem.at[number], held_sem.at[number],
                    device_id=device(0), device_id_type=MESH,
                ).wait_recv()
            for number, (par, edge, hi) in enumerate(sites):
                for idx in range(half):
                    far_panel, far_edge, turn = (seam[i, edge, 2 * idx + par] for i in range(3))
                    far_hi = hi + turn - 2 * hi * turn
                    source = ((far_panel % 2) * 4 + far_edge) * 2 + far_hi
                    chosen[number * half + idx] = held[source * half + far_panel // 2]
                to_site(number).start()
            for number in range(len(sites)):
                to_site(number).wait_send()

    for key in on_edge:
        par, edge = key
        pltpu.make_async_remote_copy(
            strips.at[par, edge], ghosts.at[par, edge],
            send_sem.at[par * 4 + edge], ghost_sem.at[par * 4 + edge],
            device_id=device(near[key]), device_id_type=MESH,
        ).wait_recv()

    for p in range(panels):
        par, idx = p % 2, p // 2
        first = PAD + p * block

        def beyond(edge, d):
            return ghosts[par, edge, idx, pl.ds(d * levels, levels), :]

        def own(edge, d):
            return strips[par, edge, idx, pl.ds(d * levels, levels), :]

        low = [beyond(0, d) - own(2, d) for d in range(2)]
        high = [beyond(2, d) - own(0, d) for d in range(2)]
        for m, value in enumerate(
            (-high[0], 8.0 * high[0] - high[1], low[1] - 8.0 * low[0], low[0])
        ):
            xb[pl.ds(m, levels, stride=4), :] = value
        tt[p] = jnp.transpose(xb[...])

        low = [beyond(3, d) - q[pl.ds(first - 1 - d, levels, stride=size), :] for d in range(2)]
        high = [beyond(1, d) - q[pl.ds(first + size + d, levels, stride=size), :] for d in range(2)]
        base = p * 2 * levels * 8
        gi[pl.ds(base, levels, stride=8), :] = low[1] - 8.0 * low[0]
        gi[pl.ds(base + 1, levels, stride=8), :] = low[0]
        base = base + levels * 8
        gi[pl.ds(base + 6, levels, stride=8), :] = -high[0]
        gi[pl.ds(base + 7, levels, stride=8), :] = 8.0 * high[0] - high[1]

        for k in range(levels):
            for last in range(2):
                here = pl.ds(p * block + k * size + last * (size - 8), 8)
                change = gi[pl.ds(((p * 2 + last) * levels + k) * 8, 8), :]
                fv[here, :] = fv[here, :] - vv[here, :] * change

    def finish(step, carry):
        p = step // (size // 16)
        i = lax.rem(step, size // 16)
        fix = tt[p, pl.ds(pl.multiple_of(i * 16, 16), 16), :]
        values, places = [], []
        for k in range(levels):
            here = pl.ds(pl.multiple_of(p * block + k * size + i * 16, 16), 16)
            value = fv[here, :] - wv[here, :] * pltpu.roll(fix, size - (4 * k + 2), 1)
            if k:
                value = value + bv[here, :] * values[-1]
            values.append(value)
            places.append(here)
        above = values[-1]
        out[places[-1], :] = above
        for k in range(levels - 2, -1, -1):
            above = values[k] + rv[places[k], :] * above
            out[places[k], :] = above
        return carry

    lax.fori_loop(0, panels * (size // 16), finish, 0)

    for key in on_edge:
        @pl.when(on_edge[key])
        def _(key=key):
            to_hub(key).wait_send()

        @pl.when(jnp.logical_not(on_edge[key]))
        def _(key=key):
            to_near(key).wait_send()


def shards(plan, tracer, east, north, diff, seam):
    _, panels, levels, size, _ = tracer.shape
    dims = panels, levels, size
    total = panels * levels * size
    half = panels // 2
    f32, bf16 = jnp.float32, jnp.bfloat16
    anywhere = pl.BlockSpec(memory_space=pltpu.HBM)
    edge_set = pltpu.VMEM((2, 4, half, 2 * levels, size), f32)
    hub_set = pltpu.VMEM((16 * half, 2 * levels, size), f32)
    whole = pltpu.VMEM((total, size), f32)
    updated = pl.pallas_call(
        functools.partial(kernel, plan, dims),
        out_shape=pltpu.VMEM((total, size), f32),
        in_specs=[anywhere] * 4 + [pl.BlockSpec(memory_space=pltpu.SMEM)],
        out_specs=pl.BlockSpec(memory_space=pltpu.VMEM),
        scratch_shapes=[
            pltpu.VMEM((total + 2 * PAD, size), f32),
            *[pltpu.VMEM((total, size), bf16)] * 3,
            *[whole] * 5,
            *[edge_set] * 3,
            *[hub_set] * 2,
            pltpu.VMEM((panels * 2 * levels * 8, size), f32),
            pltpu.VMEM((size, size), f32),
            pltpu.VMEM((panels, size, size), f32),
            pltpu.SemaphoreType.DMA((panels,)),
            pltpu.SemaphoreType.DMA((panels, 3)),
            pltpu.SemaphoreType.DMA((8,)),
            pltpu.SemaphoreType.DMA((8,)),
            pltpu.SemaphoreType.DMA((16,)),
            pltpu.SemaphoreType.DMA((16,)),
        ],
        compiler_params=pltpu.CompilerParams(
            collective_id=0, has_side_effects=True, vmem_limit_bytes=40 * 1024 * 1024
        ),
        name="transport",
    )(
        *[
            pltpu.with_memory_space_constraint(value, pltpu.HBM)
            for value in (
                *[field.reshape(total, size) for field in (tracer, east, north, diff)],
                jnp.transpose(seam, (2, 1, 0)),
            )
        ]
    )
    return updated.reshape(tracer.shape)


def solution(mesh):
    plan = Plan(mesh.shape["tile"])
    spread = P(("groups", "tile"), None, None, None, None)
    return jax.shard_map(
        functools.partial(shards, plan),
        mesh=mesh,
        in_specs=(spread, spread, spread, spread, P()),
        out_specs=spread,
        check_vma=False,
    )
```

time: 222 us -> 58.6 us (0.26)
  waiting for transfers between devices: 126 us -> 0 us
  Pallas kernels: 0 us -> 56.8 us
  local copies, waits for them, and re-layouts: 40.5 us -> 1.67 us
  starting transfers between devices: 26.2 us -> 0 us
  other arithmetic: 15.6 us -> 0 us
  between operations: 13.7 us -> 0.01 us
    all_gather x1 -> x0, waiting for transfers between devices: 126 us -> none  [shards(): everyone = lax.all_gather(blocks[None], 'tile', axis=0, tiled=True)]
    pallas_call x0 -> x1, Pallas kernels: none -> 56.8 us  [shards(): pl.pallas_call(functools.partial(kernel, plan, dims), out_shape=pltpu.VME...]
    ppermute x4 -> x0, starting transfers between devices: 26.2 us -> none  [the longest x2 14.2 us: from_behind(): return lax.ppermute(value, axis, pairs)]
    rev x3 -> x0, local copies, waits for them, and re-layouts: 17.5 us -> none  [the longest x1 17.3 us: advance(): south_part = jnp.transpose(ghosts[:, 0, ::-1], (0, 2, 3, 1))]
    sub x1 -> x0, other arithmetic: 10 us -> none  [advance(): panels - (courant_east.astype(jnp.float32) * centered(along_first, 2) + c...]
    unnamed x18 -> x1, local copies, waits for them, and re-layouts: 9.24 us -> 1.67 us
    gather x2 -> x0, local copies, waits for them, and re-layouts: 5.83 us -> none  [the longest x1 5.14 us: shards(): jnp.take(everyone.reshape((tile_count * 24,) + blocks.shape[1:]), source_...]
    slice x4 -> x0, local copies, waits for them, and re-layouts: 5.73 us -> none  [the longest x2 5.6 us: edge_strips(): north_rows = jnp.moveaxis(panels[:, :, :, ::-1][:, :, :, :rows_deep], 3, 1)]
  transfers between devices with their start and end apart: 5 -> 0, of which waited for: 1 -> 0; matrix products, arithmetic and copies ran while one was open for 2% -> 0% of each run, Pallas kernels for 0% -> 0%
where the time goes in v1:
time: 58.6 us; the launch traced here: 58.5 us
  Pallas kernels  56.8 us (97%)
  local copies, waits for them, and re-layouts  1.67 us (3%)
    pallas_call x1, Pallas kernels, shards(): pl.pallas_call(functools.partial(kernel, plan, dims), out_shape=pltpu.VME...  56.8 us
    unnamed x1, local copies, waits for them, and re-layouts  1.67 us

profile of v1, /device:TPU:37, one launch (start us, length us, event | category | flops | bytes accessed | tf_op | source)
XLA Modules:
  0.0 58.5 jit_solution(16389854533923608400)
XLA Ops:
  0.0 56.8 %transport.1 = f32[6144,128]{1,0:T(8,128)S(1)} custom-call(f32[6144,128]{1,0:T(8,128)} %bitcast.7, bf16[6144,128]{1,0:T(8,128)(2,1)} %bitcast.8, bf16[6144,128]{1,0:T(8,128)(2,1)} %bitcast.9, bf16[6144,128]{1,0:T(8,128)(2,1)} %bitcast.10, s32[3,4,6]{2,1,0:T(4,128)} %bitcast.11), custom_call_target="tpu_custom_call" | custom-call | tf_op jit(solution)/shard_map/transport/pallas_call | solution.py:329
  56.8 1.7 %copy.7 = f32[1,6,8,128,128]{4,3,2,1,0:T(8,128)} copy(f32[1,6,8,128,128]{4,3,2,1,0:T(8,128)S(1)} %bitcast.6) | data formatting | bytes 6291456

commit v2 on v1

v2 whole, which is shorter than its diff:
```python
import functools
import math

import jax
import jax.numpy as jnp
from jax import lax
from jax.experimental import pallas as pl
from jax.experimental.pallas import tpu as pltpu
from jax.sharding import PartitionSpec as P

MESH = pl.DeviceIdType.MESH
PAD = 8


class Plan:
    def __init__(self, count):
        self.count = count
        self.side = math.isqrt(count)
        self.shift = count // 2 + 1
        taken = []
        for group in range(self.side // 2):
            members = {self.site(*place) for place in self.places(group)}
            taken.append(
                next(d for d in range(1, count, 2) if d not in members and d not in taken)
            )
        self.hubs = taken

    def places(self, group):
        spots = group, self.side - 1 - group
        return [(par, edge, spot) for par in range(2) for edge in range(4) for spot in spots]

    def order(self, group):
        homes = [self.site(*place) for place in self.places(group)]
        return sorted(range(len(homes)), key=lambda i: (homes[i] >= 3 * self.count // 4, homes[i]))

    def site(self, par, edge, spot):
        side = self.side
        tile = (spot * side, (side - 1) * side + spot, spot * side + side - 1, spot)[edge]
        return (tile + self.shift * par) % self.count

    def hub_of(self, group):
        found = self.hubs[0]
        for i, hub in enumerate(self.hubs):
            if i:
                found = jnp.where(group == i, hub, found)
        return found


def kernel(
    plan, dims,
    tracer, slabs, east, north, diff, table, out,
    seam, rim, q, ce, cn, df, fv, wv, vv, bv, rv,
    strips, turned, ghosts, held, chosen, gi, xb, tt,
    table_sem, rim_sem, load_sem, coef_sem, send_sem, ghost_sem, held_sem, chosen_sem,
):
    panels, levels, size = dims
    count, side = plan.count, plan.side
    block = levels * size
    me = lax.axis_index("tile")
    half = panels // 2

    def device(d):
        return {"tile": d}

    tiles = [lax.rem(me + (count - plan.shift) * par, count) for par in range(2)]
    rows = [t // side for t in tiles]
    cols = [lax.rem(t, side) for t in tiles]
    on_edge, below, above_me, slot, hub, near = {}, {}, {}, {}, {}, {}
    for par in range(2):
        for edge in range(4):
            key = par, edge
            on_edge[key] = (
                cols[par] == 0, rows[par] == side - 1, cols[par] == side - 1, rows[par] == 0
            )[edge]
            spot = (rows, cols, rows, cols)[edge][par]
            group = jnp.minimum(spot, side - 1 - spot)
            slot[key] = (par * 4 + edge) * 2 + jnp.where(spot == group, 0, 1)
            hub[key] = plan.hub_of(group)
            near[key] = lax.rem(me + (count - 1, side, 1, count - side)[edge], count)
            inside = jnp.logical_not(on_edge[key])
            below[key] = jnp.logical_and(inside, near[key] < me)
            above_me[key] = jnp.logical_and(inside, near[key] > me)

    barrier = pltpu.get_barrier_semaphore()
    expected = 0
    for key in on_edge:
        expected = expected + jnp.where(jnp.logical_or(on_edge[key], below[key]), 1, 0)

        @pl.when(above_me[key])
        def _(key=key):
            pl.semaphore_signal(
                barrier, inc=1, device_id=device(near[key]), device_id_type=MESH
            )
    for group, hub_device in enumerate(plan.hubs):
        @pl.when(me == hub_device)
        def _(group=group):
            for place in plan.places(group):
                pl.semaphore_signal(
                    barrier, inc=1, device_id=device(plan.site(*place)), device_id_type=MESH
                )

    table_load = pltpu.make_async_copy(table, seam, table_sem)
    table_load.start()
    rim_loads = [
        pltpu.make_async_copy(slabs.at[:, pl.ds(start, 8), :], rim.at[i], rim_sem.at[i])
        for i, start in enumerate((0, size - 8))
    ]
    for load in rim_loads:
        load.start()
    loads = []
    for p in range(panels):
        load = pltpu.make_async_copy(
            tracer.at[pl.ds(p * block, block)], q.at[pl.ds(PAD + p * block, block)],
            load_sem.at[p],
        )
        load.start()
        loads.append(load)
    coefs = [
        pltpu.make_async_copy(
            far.at[pl.ds(p * block, block)], close.at[pl.ds(p * block, block)],
            coef_sem.at[p, i],
        )
        for p in range(panels)
        for i, (far, close) in enumerate(((east, ce), (north, cn), (diff, df)))
    ]

    zero = jnp.zeros((8, size), jnp.float32)
    q[pl.ds(0, PAD), :] = zero
    q[pl.ds(PAD + panels * block, PAD), :] = zero
    gi[...] = jnp.zeros(gi.shape, jnp.float32)
    xb[...] = jnp.zeros(xb.shape, jnp.float32)
    lane = lax.broadcasted_iota(jnp.int32, (8, size), 1)
    back = size - 1 - lax.broadcasted_iota(jnp.int32, (2 * levels, size), 1)

    def turn_strips(p, edges):
        par, idx = p % 2, p // 2
        for edge in edges:
            plain = strips[par, edge, idx]
            flipped = jnp.take_along_axis(plain, back, axis=1)
            turned[par, edge, idx] = jnp.where(seam[2, edge, p] == 1, flipped, plain)

    for load in rim_loads:
        load.wait()
    table_load.wait()
    for p in range(panels):
        par, idx = p % 2, p // 2
        for d in range(2):
            part = pl.ds(d * levels, levels)
            strips[par, 3, idx, part, :] = rim[0, pl.ds(p * levels, levels), d, :]
            strips[par, 1, idx, part, :] = rim[1, pl.ds(p * levels, levels), 7 - d, :]
    for p in range(panels):
        turn_strips(p, (1, 3))

    def to_hub(key):
        par, edge = key
        return pltpu.make_async_remote_copy(
            turned.at[par, edge], held.at[pl.ds(slot[key] * half, half)],
            send_sem.at[par * 4 + edge], held_sem.at[slot[key]],
            device_id=device(hub[key]), device_id_type=MESH,
        )

    def to_near(key):
        par, edge = key
        return pltpu.make_async_remote_copy(
            strips.at[par, edge], ghosts.at[par, (edge + 2) % 4],
            send_sem.at[par * 4 + edge], ghost_sem.at[par * 4 + (edge + 2) % 4],
            device_id=device(near[key]), device_id_type=MESH,
        )

    def arrival(par, edge):
        return pltpu.make_async_remote_copy(
            strips.at[par, edge], ghosts.at[par, edge],
            send_sem.at[par * 4 + edge], ghost_sem.at[par * 4 + edge],
            device_id=device(0), device_id_type=MESH,
        )

    def send(edges):
        keys = [(par, edge) for edge in edges for par in range(2)]
        for key in keys:
            @pl.when(on_edge[key])
            def _(key=key):
                to_hub(key).start()

        for key in keys:
            @pl.when(below[key])
            def _(key=key):
                to_near(key).start()

    pl.semaphore_wait(barrier, expected)
    send((1, 3))

    for load in loads:
        load.wait()
    for load in coefs:
        load.start()
    part_of = lane // 4
    for p in range(panels):
        for i in range(size // 8):
            packed = jnp.zeros((8, size), jnp.float32)
            for k in range(levels):
                moved = pltpu.roll(
                    q[pl.ds(PAD + p * block + k * size + i * 8, 8), :], 4 * k + 2, 1
                )
                packed = jnp.where(part_of == k, moved, packed)
            tt[p, pl.ds(i * 8, 8), :] = packed
    for p in range(panels):
        tt[p] = jnp.transpose(tt[p])
    for p in range(panels):
        par, idx = p % 2, p // 2
        for d in range(2):
            part = pl.ds(d * levels, levels)
            strips[par, 0, idx, part, :] = tt[p, pl.ds(2 + d, levels, stride=4), :]
            strips[par, 2, idx, part, :] = tt[p, pl.ds(1 - d, levels, stride=4), :]
    for p in range(panels):
        turn_strips(p, (0, 2))

    send((0, 2))

    twelfth = 1.0 / 12.0
    wide = lax.broadcasted_iota(jnp.int32, (16, size), 1)
    edge_lane = jnp.logical_or(wide < 2, wide >= size - 2)

    for p in range(panels):
        for load in coefs[3 * p : 3 * p + 3]:
            load.wait()

        def prepare(i, carry):
            before = ratio = None
            for k in range(levels):
                row = pl.multiple_of(p * block + k * size + i * 16, 16)
                here = pl.ds(row, 16)
                mid = q[pl.ds(row + PAD, 16), :]
                di = 8.0 * (q[pl.ds(row + PAD + 1, 16), :] - q[pl.ds(row + PAD - 1, 16), :]) - (
                    q[pl.ds(row + PAD + 2, 16), :] - q[pl.ds(row + PAD - 2, 16), :]
                )
                dj = 8.0 * (pltpu.roll(mid, size - 1, 1) - pltpu.roll(mid, 1, 1)) - (
                    pltpu.roll(mid, size - 2, 1) - pltpu.roll(mid, 2, 1)
                )
                e = ce[here, :].astype(jnp.float32) * twelfth
                n = cn[here, :].astype(jnp.float32) * twelfth
                c = df[here, :].astype(jnp.float32)
                pivot = 1.0 + c
                if k:
                    pivot = pivot + before * (1.0 - ratio)
                inv = 1.0 / pivot
                fv[here, :] = (mid - (e * di + n * dj)) * inv
                wv[here, :] = jnp.where(edge_lane, n * inv, 0.0)
                vv[here, :] = e * inv
                if k:
                    bv[here, :] = before * inv
                ratio = c * inv
                rv[here, :] = ratio
                before = c
            return carry

        lax.fori_loop(0, size // 16, prepare, 0)

    def send_up(around):
        for key in on_edge:
            far = near[key] - me > count // 2
            @pl.when(jnp.logical_and(above_me[key], far if around else jnp.logical_not(far)))
            def _(key=key):
                arrival(*key).wait_recv()
                to_near(key).start()

    send_up(False)

    def to_site(group, i):
        par, edge, _ = place = plan.places(group)[i]
        return pltpu.make_async_remote_copy(
            chosen.at[pl.ds(i * half, half)], ghosts.at[par, edge],
            chosen_sem.at[i], ghost_sem.at[par * 4 + edge],
            device_id=device(plan.site(*place)), device_id_type=MESH,
        )

    for group, hub_device in enumerate(plan.hubs):
        @pl.when(me == hub_device)
        def _(group=group):
            places = plan.places(group)
            for i in range(len(places)):
                pltpu.make_async_remote_copy(
                    held.at[pl.ds(i * half, half)], held.at[pl.ds(i * half, half)],
                    chosen_sem.at[i], held_sem.at[i],
                    device_id=device(0), device_id_type=MESH,
                ).wait_recv()
            for i in plan.order(group):
                par, edge, spot = places[i]
                mirrored = int(spot != group)
                for idx in range(half):
                    far_panel, far_edge, turn = (seam[j, edge, 2 * idx + par] for j in range(3))
                    far_mirrored = mirrored + turn - 2 * mirrored * turn
                    source = ((far_panel % 2) * 4 + far_edge) * 2 + far_mirrored
                    chosen[i * half + idx] = held[source * half + far_panel // 2]
                to_site(group, i).start()

    send_up(True)

    bent = functools.reduce(jnp.logical_or, [on_edge[0, edge] for edge in range(4)])

    def solve(par):
        for edge in range(4):
            late = jnp.logical_not(jnp.where(par == 0, above_me[0, edge], above_me[1, edge]))

            @pl.when(late)
            def _(edge=edge):
                arrival(par, edge).wait_recv()

        for idx in range(half):
            p = 2 * idx + par
            first = pl.multiple_of(PAD + p * block, 8)

            def beyond(edge, d):
                return ghosts[par, edge, idx, pl.ds(d * levels, levels), :]

            def own(edge, d):
                return strips[par, edge, idx, pl.ds(d * levels, levels), :]

            low = [beyond(0, d) - own(2, d) for d in range(2)]
            high = [beyond(2, d) - own(0, d) for d in range(2)]
            for m, value in enumerate(
                (-high[0], 8.0 * high[0] - high[1], low[1] - 8.0 * low[0], low[0])
            ):
                xb[idx, pl.ds(m, levels, stride=4), :] = value

            low = [
                beyond(3, d) - q[pl.ds(first - 1 - d, levels, stride=size), :] for d in range(2)
            ]
            high = [
                beyond(1, d) - q[pl.ds(first + size + d, levels, stride=size), :] for d in range(2)
            ]
            base = idx * 2 * levels * 8
            gi[pl.ds(base, levels, stride=8), :] = low[1] - 8.0 * low[0]
            gi[pl.ds(base + 1, levels, stride=8), :] = low[0]
            base = base + levels * 8
            gi[pl.ds(base + 6, levels, stride=8), :] = -high[0]
            gi[pl.ds(base + 7, levels, stride=8), :] = 8.0 * high[0] - high[1]
        for idx in range(half):
            tt[idx] = jnp.transpose(xb[idx])
        for idx in range(half):
            start = (2 * idx + par) * block
            for k in range(levels):
                for last in range(2):
                    here = pl.ds(pl.multiple_of(start + k * size + last * (size - 8), 8), 8)
                    change = gi[pl.ds(((idx * 2 + last) * levels + k) * 8, 8), :]
                    fv[here, :] = fv[here, :] - vv[here, :] * change

        def finish(step, carry):
            idx = step // (size // 16)
            i = lax.rem(step, size // 16)
            fix = tt[idx, pl.ds(pl.multiple_of(i * 16, 16), 16), :]
            values, places = [], []
            for k in range(levels):
                row = (2 * idx + par) * block + k * size + i * 16
                here = pl.ds(pl.multiple_of(row, 16), 16)
                value = fv[here, :] - wv[here, :] * pltpu.roll(fix, size - (4 * k + 2), 1)
                if k:
                    value = value + bv[here, :] * values[-1]
                values.append(value)
                places.append(here)
            upper = values[-1]
            out[places[-1], :] = upper
            for k in range(levels - 2, -1, -1):
                upper = values[k] + rv[places[k], :] * upper
                out[places[k], :] = upper
            return carry

        lax.fori_loop(0, half * (size // 16), finish, 0, unroll=4)

    @pl.loop(0, 2)
    def _(turn):
        solve(jnp.where(bent, 1 - turn, turn))

    for key in on_edge:
        @pl.when(on_edge[key])
        def _(key=key):
            to_hub(key).wait_send()

        @pl.when(jnp.logical_not(on_edge[key]))
        def _(key=key):
            to_near(key).wait_send()

    for group, hub_device in enumerate(plan.hubs):
        @pl.when(me == hub_device)
        def _(group=group):
            for i in plan.order(group):
                to_site(group, i).wait_send()


def shards(plan, tracer, east, north, diff, seam):
    _, panels, levels, size, _ = tracer.shape
    dims = panels, levels, size
    total = panels * levels * size
    half = panels // 2
    f32, bf16 = jnp.float32, jnp.bfloat16
    anywhere = pl.BlockSpec(memory_space=pltpu.HBM)
    edge_set = pltpu.VMEM((2, 4, half, 2 * levels, size), f32)
    hub_set = pltpu.VMEM((16 * half, 2 * levels, size), f32)
    whole = pltpu.VMEM((total, size), f32)
    updated = pl.pallas_call(
        functools.partial(kernel, plan, dims),
        out_shape=pltpu.VMEM((total, size), f32),
        in_specs=[anywhere] * 6,
        out_specs=pl.BlockSpec(memory_space=pltpu.VMEM),
        scratch_shapes=[
            pltpu.SMEM((3, 4, panels), jnp.int32),
            pltpu.VMEM((2, panels * levels, 8, size), f32),
            pltpu.VMEM((total + 2 * PAD, size), f32),
            *[pltpu.VMEM((total, size), bf16)] * 3,
            *[whole] * 5,
            *[edge_set] * 3,
            *[hub_set] * 2,
            pltpu.VMEM((half * 2 * levels * 8, size), f32),
            pltpu.VMEM((half, size, size), f32),
            pltpu.VMEM((panels, size, size), f32),
            pltpu.SemaphoreType.DMA,
            pltpu.SemaphoreType.DMA((2,)),
            pltpu.SemaphoreType.DMA((panels,)),
            pltpu.SemaphoreType.DMA((panels, 3)),
            pltpu.SemaphoreType.DMA((8,)),
            pltpu.SemaphoreType.DMA((8,)),
            pltpu.SemaphoreType.DMA((16,)),
            pltpu.SemaphoreType.DMA((16,)),
        ],
        compiler_params=pltpu.CompilerParams(
            collective_id=0, has_side_effects=True, vmem_limit_bytes=40 * 1024 * 1024
        ),
        name="transport",
    )(
        *[
            pltpu.with_memory_space_constraint(value, pltpu.HBM)
            for value in (
                tracer.reshape(total, size),
                tracer.reshape(panels * levels, size, size),
                *[field.reshape(total, size) for field in (east, north, diff)],
                jnp.transpose(seam, (2, 1, 0)),
            )
        ]
    )
    return updated.reshape(tracer.shape)


def solution(mesh):
    plan = Plan(mesh.shape["tile"])
    spread = P(("groups", "tile"), None, None, None, None)
    return jax.shard_map(
        functools.partial(shards, plan),
        mesh=mesh,
        in_specs=(spread, spread, spread, spread, P()),
        out_specs=spread,
        check_vma=False,
    )
```

time: 58.6 us -> 48.3 us (0.82)
  Pallas kernels: 56.8 us -> 46.5 us
    pallas_call x1, Pallas kernels: 56.8 us -> 46.5 us  [shards(): pl.pallas_call(functools.partial(kernel, plan, dims), out_shape=pltpu.VME...]
where the time goes in v2:
time: 48.3 us; the launch traced here: 48.2 us
  Pallas kernels  46.5 us (96%)
  local copies, waits for them, and re-layouts  1.67 us (3%)
    pallas_call x1, Pallas kernels, shards(): pl.pallas_call(functools.partial(kernel, plan, dims), out_shape=pltpu.VME...  46.5 us
    unnamed x1, local copies, waits for them, and re-layouts  1.67 us

profile of v2, /device:TPU:37, one launch (start us, length us, event | category | flops | bytes accessed | tf_op | source)
XLA Modules:
  0.0 48.2 jit_solution(13513885953835084311)
XLA Ops:
  0.0 46.5 %transport.1 = f32[6144,128]{1,0:T(8,128)S(1)} custom-call(f32[6144,128]{1,0:T(8,128)} %bitcast.8, f32[48,128,128]{2,1,0:T(8,128)} %bitcast.9, bf16[6144,128]{1,0:T(8,128)(2,1)} %bitcast.10, bf16[6144,128]{1,0:T(8,128)(2,1)} %bitcast.11, bf16[6144,128]{1,0:T(8,128)(2,1)} %bitcast.12, s32[3,4,6]{2,1,0:T(4,128)} %bitcast.13), custom_call_target="tpu_custom_call" | custom-call | tf_op jit(solution)/shard_map/transport/pallas_call | solution.py:399
  46.6 1.7 %copy.7 = f32[1,6,8,128,128]{4,3,2,1,0:T(8,128)} copy(f32[1,6,8,128,128]{4,3,2,1,0:T(8,128)S(1)} %bitcast.7) | data formatting | bytes 6291456

commit v3 on v2

--- a/solution.py
+++ b/solution.py
@@ -21,7 +21,7 @@
         for group in range(self.side // 2):
             members = {self.site(*place) for place in self.places(group)}
             taken.append(
-                next(d for d in range(1, count, 2) if d not in members and d not in taken)
+                next(d for d in range(5, count, 2) if d not in members and d not in taken)
             )
         self.hubs = taken
 
@@ -29,9 +29,11 @@
         spots = group, self.side - 1 - group
         return [(par, edge, spot) for par in range(2) for edge in range(4) for spot in spots]
 
-    def order(self, group):
+    def waves(self, group):
         homes = [self.site(*place) for place in self.places(group)]
-        return sorted(range(len(homes)), key=lambda i: (homes[i] >= 3 * self.count // 4, homes[i]))
+        inner = sorted(range(len(homes)), key=lambda i: homes[i])
+        first = [i for i in inner if homes[i] < self.count // 4]
+        return first, [i for i in inner if i not in first]
 
     def site(self, par, edge, spot):
         side = self.side
@@ -283,7 +285,12 @@
                     chosen_sem.at[i], held_sem.at[i],
                     device_id=device(0), device_id_type=MESH,
                 ).wait_recv()
-            for i in plan.order(group):
+            first, rest = plan.waves(group)
+            for i in first + [None] + rest:
+                if i is None:
+                    for j in first:
+                        to_site(group, j).wait_send()
+                    continue
                 par, edge, spot = places[i]
                 mirrored = int(spot != group)
                 for idx in range(half):
@@ -364,7 +371,7 @@
                 out[places[k], :] = upper
             return carry
 
-        lax.fori_loop(0, half * (size // 16), finish, 0, unroll=4)
+        lax.fori_loop(0, half * (size // 16), finish, 0, unroll=8)
 
     @pl.loop(0, 2)
     def _(turn):
@@ -382,7 +389,7 @@
     for group, hub_device in enumerate(plan.hubs):
         @pl.when(me == hub_device)
         def _(group=group):
-            for i in plan.order(group):
+            for i in plan.waves(group)[1]:
                 to_site(group, i).wait_send()
 
 

time: 48.3 us -> 45.8 us (0.948)
  Pallas kernels: 46.5 us -> 44 us
    pallas_call x1, Pallas kernels: 46.5 us -> 44 us  [shards(): pl.pallas_call(functools.partial(kernel, plan, dims), out_shape=pltpu.VME...]
where the time goes in v3:
time: 45.8 us; the launch traced here: 45.6 us
  Pallas kernels  44 us (96%)
  local copies, waits for them, and re-layouts  1.67 us (4%)
    pallas_call x1, Pallas kernels, shards(): pl.pallas_call(functools.partial(kernel, plan, dims), out_shape=pltpu.VME...  44 us
    unnamed x1, local copies, waits for them, and re-layouts  1.67 us

profile of v3, /device:TPU:37, one launch (start us, length us, event | category | flops | bytes accessed | tf_op | source)
XLA Modules:
  0.0 45.6 jit_solution(12066379366232871791)
XLA Ops:
  0.0 44.0 %transport.1 = f32[6144,128]{1,0:T(8,128)S(1)} custom-call(f32[6144,128]{1,0:T(8,128)} %bitcast.8, f32[48,128,128]{2,1,0:T(8,128)} %bitcast.9, bf16[6144,128]{1,0:T(8,128)(2,1)} %bitcast.10, bf16[6144,128]{1,0:T(8,128)(2,1)} %bitcast.11, bf16[6144,128]{1,0:T(8,128)(2,1)} %bitcast.12, s32[3,4,6]{2,1,0:T(4,128)} %bitcast.13), custom_call_target="tpu_custom_call" | custom-call | tf_op jit(solution)/shard_map/transport/pallas_call | solution.py:406
  44.0 1.7 %copy.7 = f32[1,6,8,128,128]{4,3,2,1,0:T(8,128)} copy(f32[1,6,8,128,128]{4,3,2,1,0:T(8,128)S(1)} %bitcast.7) | data formatting | bytes 6291456

commit v4 on v3

--- a/solution.py
+++ b/solution.py
@@ -32,8 +32,10 @@
     def waves(self, group):
         homes = [self.site(*place) for place in self.places(group)]
         inner = sorted(range(len(homes)), key=lambda i: homes[i])
-        first = [i for i in inner if homes[i] < self.count // 4]
-        return first, [i for i in inner if i not in first]
+        near = [i for i in inner if homes[i] < self.count // 4]
+        ahead = [i for i in inner if self.count // 4 <= homes[i] < self.count // 2 + 6]
+        behind = [i for i in inner if i not in near + ahead]
+        return [near, ahead + behind] if group == 0 else [near, ahead, behind]
 
     def site(self, par, edge, spot):
         side = self.side
@@ -285,12 +287,14 @@
                     chosen_sem.at[i], held_sem.at[i],
                     device_id=device(0), device_id_type=MESH,
                 ).wait_recv()
-            first, rest = plan.waves(group)
-            for i in first + [None] + rest:
-                if i is None:
-                    for j in first:
+            waves = plan.waves(group)
+            steps = [(number, i) for number, wave in enumerate(waves) for i in wave]
+            sent = 0
+            for number, i in steps:
+                while sent < number:
+                    for j in waves[sent]:
                         to_site(group, j).wait_send()
-                    continue
+                    sent += 1
                 par, edge, spot = places[i]
                 mirrored = int(spot != group)
                 for idx in range(half):
@@ -389,7 +393,7 @@
     for group, hub_device in enumerate(plan.hubs):
         @pl.when(me == hub_device)
         def _(group=group):
-            for i in plan.waves(group)[1]:
+            for i in plan.waves(group)[-1]:
                 to_site(group, i).wait_send()
 
 

time: 45.8 us -> 45.6 us (level)
  no operation moved by 1% of the time
where the time goes in v4:
time: 45.6 us; the launch traced here: 45.5 us
  Pallas kernels  43.8 us (96%)
  local copies, waits for them, and re-layouts  1.67 us (4%)
    pallas_call x1, Pallas kernels, shards(): pl.pallas_call(functools.partial(kernel, plan, dims), out_shape=pltpu.VME...  43.8 us
    unnamed x1, local copies, waits for them, and re-layouts  1.67 us

profile of v4, /device:TPU:37, one launch (start us, length us, event | category | flops | bytes accessed | tf_op | source)
XLA Modules:
  0.0 45.5 jit_solution(2446630716177082586)
XLA Ops:
  0.0 43.8 %transport.1 = f32[6144,128]{1,0:T(8,128)S(1)} custom-call(f32[6144,128]{1,0:T(8,128)} %bitcast.8, f32[48,128,128]{2,1,0:T(8,128)} %bitcast.9, bf16[6144,128]{1,0:T(8,128)(2,1)} %bitcast.10, bf16[6144,128]{1,0:T(8,128)(2,1)} %bitcast.11, bf16[6144,128]{1,0:T(8,128)(2,1)} %bitcast.12, s32[3,4,6]{2,1,0:T(4,128)} %bitcast.13), custom_call_target="tpu_custom_call" | custom-call | tf_op jit(solution)/shard_map/transport/pallas_call | solution.py:410
  43.8 1.7 %copy.7 = f32[1,6,8,128,128]{4,3,2,1,0:T(8,128)} copy(f32[1,6,8,128,128]{4,3,2,1,0:T(8,128)S(1)} %bitcast.7) | data formatting | bytes 6291456

commit v5 on v4

--- a/solution.py
+++ b/solution.py
@@ -415,12 +415,12 @@
         scratch_shapes=[
             pltpu.SMEM((3, 4, panels), jnp.int32),
             pltpu.VMEM((2, panels * levels, 8, size), f32),
-            pltpu.VMEM((total + 2 * PAD, size), f32),
+            pltpu.VMEM((total + PAD + 2 * size, size), f32),
             *[pltpu.VMEM((total, size), bf16)] * 3,
             *[whole] * 5,
             *[edge_set] * 3,
             *[hub_set] * 2,
-            pltpu.VMEM((half * 2 * levels * 8, size), f32),
+            pltpu.VMEM(((half * 2 + 1) * levels * 8, size), f32),
             pltpu.VMEM((half, size, size), f32),
             pltpu.VMEM((panels, size, size), f32),
             pltpu.SemaphoreType.DMA,

time: 45.6 us -> 45.6 us (level)
  no operation moved by 1% of the time
where the time goes in v5:
time: 45.6 us; the launch traced here: 45.5 us
  Pallas kernels  43.8 us (96%)
  local copies, waits for them, and re-layouts  1.67 us (4%)
    pallas_call x1, Pallas kernels, shards(): pl.pallas_call(functools.partial(kernel, plan, dims), out_shape=pltpu.VME...  43.8 us
    unnamed x1, local copies, waits for them, and re-layouts  1.67 us

profile of v5, /device:TPU:37, one launch (start us, length us, event | category | flops | bytes accessed | tf_op | source)
XLA Modules:
  0.0 45.5 jit_solution(1326469987922272310)
XLA Ops:
  0.0 43.8 %transport.1 = f32[6144,128]{1,0:T(8,128)S(1)} custom-call(f32[6144,128]{1,0:T(8,128)} %bitcast.8, f32[48,128,128]{2,1,0:T(8,128)} %bitcast.9, bf16[6144,128]{1,0:T(8,128)(2,1)} %bitcast.10, bf16[6144,128]{1,0:T(8,128)(2,1)} %bitcast.11, bf16[6144,128]{1,0:T(8,128)(2,1)} %bitcast.12, s32[3,4,6]{2,1,0:T(4,128)} %bitcast.13), custom_call_target="tpu_custom_call" | custom-call | tf_op jit(solution)/shard_map/transport/pallas_call | solution.py:410
  43.8 1.7 %copy.7 = f32[1,6,8,128,128]{4,3,2,1,0:T(8,128)} copy(f32[1,6,8,128,128]{4,3,2,1,0:T(8,128)S(1)} %bitcast.7) | data formatting | bytes 6291456
